TPU v7x, 32 devices: a whole 2x2x4 slice. The times are simulated.
32 devices in a mesh: groups: 2 (over y), tensor: 4 (over z), frames: 4 (over x, core).
Axes of the slice: x: 2, y: 2, z: 4, core: 2. Of those that a mesh axis runs over, the one named last changes fastest.
Arguments:
- patches: bfloat16 [256, 16, 3072], P('tensor', ('groups', 'frames')), parts along dimension 1, may hold values from -12 to 12
- ln_gain: float32 [3072], replicated, may hold values from 0.5 to 1.5
- in_weight: bfloat16 [3072, 4, 768], P('frames', 'tensor'), may hold values from -0.109375 to 0.109375
- q_gain: float32 [4, 128], P('tensor'), may hold values from 0.1 to 1.9
- k_gain: float32 [4, 128], P('tensor'), may hold values from 0.1 to 1.9
- out_weight: bfloat16 [4, 512, 3072], P('tensor', None, 'frames'), may hold values from -0.25 to 0.25
Outputs:
- encoded: bfloat16 [256, 16, 3072], P('tensor', ('groups', 'frames')), parts along dimension 1
There are 2 independent parts, one for each index of `groups`. A program takes and returns all parts, laid end to end along the dimension named above; an argument that names none is the same for every part. Nothing has to cross between parts.
All inputs are finite; a program needn't handle non-finite values.
Results may differ from a plain program's by a relative error of at most 0.022.
Values may be sent and summed in bfloat16 or wider, within the bound.
No kernel may reach another device: no remote copies, remote signals or barrier semaphores. Data moves between devices by JAX's collectives and lax.ppermute only.
A program may use at most 64 MiB of HBM per device.

v0:
```python
import math
import jax
import jax.numpy as jnp
from jax import lax
from jax.sharding import PartitionSpec as P


def layer_norm(values, gain_vec):
    mean_val = jnp.mean(values, axis=-1, keepdims=True)
    centered = values - mean_val
    variance = jnp.mean(centered * centered, axis=-1, keepdims=True)
    return centered * lax.rsqrt(variance + 1e-06) * gain_vec


def local(patches, ln_gain, in_weight, q_gain, k_gain, out_weight):
    head_dim = q_gain.shape[1]
    normed = layer_norm(patches.astype(jnp.float32), ln_gain).astype(jnp.bfloat16)
    in_local = in_weight[:, 0, :]
    out_local = out_weight[0]
    every_patch = lax.all_gather(normed, "tensor", axis=0, tiled=True)
    joined_cols = jnp.einsum(
        "qye,ea->qya",
        every_patch,
        lax.all_gather(in_local, "frames", axis=0, tiled=True),
        preferred_element_type=jnp.float32,
    )
    query_slice = layer_norm(joined_cols[..., :head_dim], q_gain[0])
    key_slice = layer_norm(joined_cols[..., head_dim : 2 * head_dim], k_gain[0])
    value_slice = joined_cols[..., 2 * head_dim : 3 * head_dim]
    hidden = jax.nn.gelu(joined_cols[..., 3 * head_dim :], approximate=False)
    prepared = jnp.concatenate([query_slice, key_slice, value_slice, hidden], axis=-1).astype(
        jnp.bfloat16
    )
    query_slice = prepared[..., :head_dim]
    key_slice = prepared[..., head_dim : 2 * head_dim]
    value_slice = prepared[..., 2 * head_dim : 3 * head_dim]
    attention_logits = jnp.einsum(
        "ldg,bdg->dlb", query_slice, key_slice, preferred_element_type=jnp.float32
    ) * (1.0 / math.sqrt(head_dim))
    exponent_scores = jnp.exp(attention_logits)
    softmax_total = jnp.sum(exponent_scores, axis=-1)
    attention_output = jnp.einsum(
        "jdl,ljg->djg",
        exponent_scores.astype(jnp.bfloat16),
        value_slice,
        preferred_element_type=jnp.float32,
    )
    attention_output = attention_output / jnp.transpose(softmax_total)[:, :, None]
    blended_rows = jnp.concatenate(
        [attention_output.astype(jnp.bfloat16), prepared[..., 3 * head_dim :]], axis=-1
    )
    combined_output = lax.all_gather(out_local, "frames", axis=1, tiled=True)
    summed = lax.psum_scatter(
        jnp.einsum(
            "vto,ox->vtx", blended_rows, combined_output, preferred_element_type=jnp.float32
        ).astype(jnp.bfloat16),
        "tensor",
        scatter_dimension=0,
        tiled=True,
    ).astype(jnp.float32)
    return (patches.astype(jnp.float32) + summed).astype(jnp.bfloat16)


def solution(mesh):
    return jax.shard_map(
        local,
        mesh=mesh,
        in_specs=(
            P("tensor", ("groups", "frames"), None),
            P(),
            P("frames", "tensor", None),
            P("tensor", None),
            P("tensor", None),
            P("tensor", None, "frames"),
        ),
        out_specs=P("tensor", ("groups", "frames"), None),
        check_vma=False,
    )
```

profile of v0, /device:TPU:0, one launch (start us, length us, event | category | flops | bytes accessed | tf_op | source)
XLA Modules:
  0.0 220.3 jit_solution(9089769881547310153)
XLA Ops:
  6.5 1.4 convert_reduce_fusion
  7.9 1.5 fusion.5
  9.5 1.2 fusion.7
  10.7 0.0 all-gather.6.cloned.1.call-update
  10.7 0.0 all-gather.8.cloned.1.call-start
  10.8 0.7 all-gather.8.cloned.1.call-update
  11.5 0.0 all-gather.10.cloned.1.call-start
  11.5 0.7 all-gather.10.cloned.1.call-update
  12.2 0.0 copy-start.2
  12.2 0.0 reduce-scatter.2.cloned.1.call-start
  12.3 64.8 %all-gather.6.cloned.1.call-done = bf16[256,2,3072]{2,0,1:T(8,128)(2,1)} async-done(((bf16[64,2,3072]{2,0,1:T(8,128)(2,1)}), bf16[256,2,3072]{2,0,1:T(8,128)(2,1)}) %all-gather.6.cloned.1.call-update) | async-done | bytes 3145744 | tf_op jit(solution)/shard_map/all_gather | solution.py:20
  77.0 37.7 %all-gather.8.cloned.1.call-done = bf16[3072,1,768]{2,0,1:T(8,128)(2,1)} async-done(((bf16[768,1,768]{2,0,1:T(8,128)(2,1)}), bf16[3072,1,768]{2,0,1:T(8,128)(2,1)}) %all-gather.8.cloned.1.call-update) | async-done | bytes 4718608 | tf_op jit(solution)/shard_map/all_gather | solution.py:24
  114.7 5.9 %fusion = f32[256,2,768]{2,0,1:T(8,128)S(1)} fusion(bf16[256,2,3072]{2,0,1:T(8,128)(2,1)} %all-gather.6.cloned.1.call-done, bf16[3072,1,768]{2,0,1:T(8,128)(2,1)} %all-gather.8.cloned.1.call-done), kind=kOutput, calls=%fused_computation | convolution fusion | flops 2415919104 | bytes 9437184 | tf_op jit(solution)/shard_map/qye,ea->qya/dot_general | solution.py:21
  120.6 0.2 slice_reduce_fusion.1
  120.8 0.4 multiply_reduce_fusion.1
  121.3 0.5 fusion.33
  121.8 0.3 fusion.11
  122.0 1.7 fusion.14
  123.8 21.1 %all-gather.10.cloned.1.call-done = bf16[1,512,3072]{2,1,0:T(8,128)(2,1)} async-done(((bf16[1,512,768]{2,1,0:T(8,128)(2,1)}), bf16[1,512,3072]{2,1,0:T(8,128)(2,1)}) %all-gather.10.cloned.1.call-update) | async-done | bytes 3145744 | tf_op jit(solution)/shard_map/all_gather | solution.py:52
  144.8 5.4 %convolution_convert_fusion = bf16[256,2,3072]{2,0,1:T(8,128)(2,1)} fusion(bf16[1,512,3072]{2,1,0:T(8,128)(2,1)} %all-gather.10.cloned.1.call-done, bf16[256,2,384]{2,0,1:T(8,128)(2,1)S(1)} %fusion.14, bf16[256,2,128]{2,0,1:T(8,128)(2,1)S(1)} %fusion.11), kind=kOutput, calls=%fused_computation.2 | convolution fusion | flops 1613234176 | bytes 6815744 | tf_op jit(solution)/shard_map/vto,ox->vtx/dot_general | solution.py:54
  150.2 0.0 reduce-scatter.2.cloned.1.call-update
  150.2 60.6 %reduce-scatter.2.cloned.1.call-done = bf16[64,2,3072]{2,0,1:T(8,128)(2,1)} async-done(((bf16[256,2,3072]{2,0,1:T(8,128)(2,1)}), bf16[64,2,3072]{2,0,1:T(8,128)(2,1)}) %reduce-scatter.2.cloned.1.call-update) | async-done | bytes 786448 | tf_op jit(solution)/shard_map/reduce_scatter | solution.py:53
  210.8 1.3 fusion.8
  212.1 1.7 copy.8
  (13 shorter events, 0.1 us)
Async XLA Ops:
  6.5 2.9 %copy-start = (bf16[64,2,3072]{2,1,0:T(2,128)(2,1)S(1)}, bf16[64,2,3072]{2,1,0:T(2,128)(2,1)}, u32[]{:S(2)}) copy-start(bf16[64,2,3072]{2,1,0:T(2,128)(2,1)} %param.6) | copy-start | bytes 2359300
  6.5 2.9 %copy-start.1 = (f32[3072]{0:T(1024)S(1)}, f32[3072]{0:T(1024)}, u32[]{:S(2)}) copy-start(f32[3072]{0:T(1024)} %param.7) | copy-start | bytes 36868
  6.5 70.5 %all-gather.6.cloned.1.call-start = ((), (), s32[]{:S(2)}) async-start(), calls=%async_computation.1 | async-start | bytes 3932160 | tf_op jit(solution)/shard_map/all_gather | solution.py:20
  10.7 104.0 %all-gather.8.cloned.1.call-start = ((), (), s32[]{:S(2)}) async-start(), calls=%async_computation.3 | async-start | bytes 5898240 | tf_op jit(solution)/shard_map/all_gather | solution.py:24
  11.5 133.3 %all-gather.10.cloned.1.call-start = ((), (), s32[]{:S(2)}) async-start(), calls=%async_computation.4 | async-start | bytes 3932160 | tf_op jit(solution)/shard_map/all_gather | solution.py:52
  12.2 109.0 %copy-start.2 = (f32[1,128]{1,0:T(1,128)S(1)}, f32[1,128]{1,0:T(1,128)}, u32[]{:S(2)}) copy-start(f32[1,128]{1,0:T(1,128)} %param.10) | copy-start | bytes 1540
  12.2 109.0 %copy-start.3 = (f32[1,128]{1,0:T(1,128)S(1)}, f32[1,128]{1,0:T(1,128)}, u32[]{:S(2)}) copy-start(f32[1,128]{1,0:T(1,128)} %param.9) | copy-start | bytes 1540
  12.2 198.5 %reduce-scatter.2.cloned.1.call-start = ((), (), s32[]{:S(2)}) async-start(), calls=%async_computation.2 | async-start | bytes 3932160 | tf_op jit(solution)/shard_map/reduce_scatter | solution.py:53
Sparse Core Ops, SparseCore 0:
  10.8 66.1 all-gather.5
  78.6 36.0 all-gather.7
  116.3 28.5 all-gather.9
  150.3 60.3 reduce-scatter.1
where the time goes:
time: 221 us; the launch traced here: 220 us
  waiting for transfers between devices  185 us (84%)
  between operations  13.2 us (6%)
  matrix products  12 us (5%)
  other arithmetic  7.81 us (4%)
    all_gather x1, waiting for transfers between devices, local(): every_patch = lax.all_gather(normed, 'tensor', axis=0, tiled=True)  64.8 us
    reduce_scatter x1, waiting for transfers between devices, local(): lax.psum_scatter(jnp.einsum('vto,ox->vtx', blended_rows, combined_output,...  60.6 us
    all_gather x1, waiting for transfers between devices, local(): lax.all_gather(in_local, 'frames', axis=0, tiled=True)  37.7 us
    all_gather x1, waiting for transfers between devices, local(): combined_output = lax.all_gather(out_local, 'frames', axis=1, tiled=True)  21.1 us
    dot_general x1, matrix products, local(): jnp.einsum('qye,ea->qya', every_patch, lax.all_gather(in_local, 'frames',...  5.89 us
    dot_general x1, matrix products, local(): jnp.einsum('vto,ox->vtx', blended_rows, combined_output, preferred_elemen...  5.36 us
  transfers between devices with their start and end apart: 4, of which 4 were waited for; matrix products, arithmetic and copies ran while one was open for 4% of the time, Pallas kernels for 0%

commit v1 on v0

--- a/solution.py
+++ b/solution.py
@@ -3,6 +3,24 @@
 import jax.numpy as jnp
 from jax import lax
 from jax.sharding import PartitionSpec as P
+
+
+def ring_apply(shard, axis, dim, apply, out_dim):
+    peers, mine, rows = (lax.axis_size(axis), lax.axis_index(axis), shard.shape[dim])
+    right = [(i, (i + 1) % peers) for i in range(peers)]
+    block, result = (shard, None)
+    for turn in range(peers):
+        owner = (mine - turn) % peers
+        upcoming = lax.ppermute(block, axis, right) if turn < peers - 1 else None
+        made = apply(block, owner * rows)
+        length = made.shape[out_dim]
+        if result is None:
+            result = jnp.zeros(
+                (*made.shape[:out_dim], peers * length, *made.shape[out_dim + 1 :]), made.dtype
+            )
+        result = lax.dynamic_update_slice_in_dim(result, made, owner * length, axis=out_dim)
+        block = upcoming
+    return result
 
 
 def layer_norm(values, gain_vec):
@@ -49,10 +67,15 @@
     blended_rows = jnp.concatenate(
         [attention_output.astype(jnp.bfloat16), prepared[..., 3 * head_dim :]], axis=-1
     )
-    combined_output = lax.all_gather(out_local, "frames", axis=1, tiled=True)
     summed = lax.psum_scatter(
-        jnp.einsum(
-            "vto,ox->vtx", blended_rows, combined_output, preferred_element_type=jnp.float32
+        ring_apply(
+            out_local,
+            "frames",
+            1,
+            lambda part, offset: jnp.einsum(
+                "vto,ox->vtx", blended_rows, part, preferred_element_type=jnp.float32
+            ),
+            2,
         ).astype(jnp.bfloat16),
         "tensor",
         scatter_dimension=0,

time: 221 us -> 203 us (0.919)
  waiting for transfers between devices: 185 us -> 164 us
  local copies, waits for them, and re-layouts: 1.71 us -> 5.04 us
    ppermute x0 -> x3, waiting for transfers between devices: none -> 23.1 us  [ring_apply(): upcoming = lax.ppermute(block, axis, right) if turn < peers - 1 else None]
    all_gather x1, waiting for transfers between devices: 64.8 us -> 41.9 us  [local(): every_patch = lax.all_gather(normed, 'tensor', axis=0, tiled=True)]
    all_gather x1 -> x0, waiting for transfers between devices: 21.1 us -> none  [local(): combined_output = lax.all_gather(out_local, 'frames', axis=1, tiled=True)]
    unnamed x8 -> x18, local copies, waits for them, and re-layouts: 0.02 us -> 2.99 us
    dot_general x1 -> x4, matrix products: 5.36 us -> 4.57 us  [local(): jnp.einsum('vto,ox->vtx', blended_rows, part, preferred_element_type=jnp....]
  transfers between devices with their start and end apart: 4 -> 6, of which waited for: 4 -> 5; matrix products, arithmetic and copies ran while one was open for 4% -> 6% of each run, Pallas kernels for 0% -> 0%
where the time goes in v1:
time: 203 us; the launch traced here: 202 us
  waiting for transfers between devices  164 us (81%)
  between operations  13.3 us (7%)
  matrix products  11.2 us (6%)
  other arithmetic  8.04 us (4%)
  local copies, waits for them, and re-layouts  5.04 us (2%)
    reduce_scatter x1, waiting for transfers between devices, local(): lax.psum_scatter(ring_apply(out_local, 'frames', 1, lambda part, offset:...  60.6 us
    all_gather x1, waiting for transfers between devices, local(): every_patch = lax.all_gather(normed, 'tensor', axis=0, tiled=True)  41.9 us
    all_gather x1, waiting for transfers between devices, local(): lax.all_gather(in_local, 'frames', axis=0, tiled=True)  37.7 us
    ppermute x3, waiting for transfers between devices, ring_apply(): upcoming = lax.ppermute(block, axis, right) if turn < peers - 1 else None  23.1 us
    dot_general x1, matrix products, local(): jnp.einsum('qye,ea->qya', every_patch, lax.all_gather(in_local, 'frames',...  5.89 us
    dot_general x4, matrix products, local(): jnp.einsum('vto,ox->vtx', blended_rows, part, preferred_element_type=jnp....  4.57 us
  transfers between devices with their start and end apart: 6, of which 5 were waited for; matrix products, arithmetic and copies ran while one was open for 6% of the time, Pallas kernels for 0%

profile of v1, /device:TPU:0, one launch (start us, length us, event | category | flops | bytes accessed | tf_op | source)
XLA Modules:
  0.0 202.1 jit_solution(17286383190789408841)
XLA Ops:
  6.5 1.4 convert_reduce_fusion
  7.9 1.5 fusion.4
  9.5 1.2 fusion.6
  10.8 0.7 all-gather.6.cloned.1.call-update
  11.5 0.5 collective-permute-start
  12.1 11.6 %collective-permute-done = bf16[512,768]{1,0:T(8,128)(2,1)S(1)} collective-permute-done((bf16[512,768]{1,0:T(8,128)(2,1)S(1)}, bf16[512,768]{1,0:T(8,128)(2,1)S(1)}, u32[]{:S(2)}, u32[]{:S(2)}) %collective-permute-start) | collective-permute-done | bytes 786464 | tf_op jit(solution)/shard_map/ppermute | solution.py:14
  23.7 11.5 %collective-permute-done.1 = bf16[512,768]{1,0:T(8,128)(2,1)} collective-permute-done((bf16[512,768]{1,0:T(8,128)(2,1)S(1)}, bf16[512,768]{1,0:T(8,128)(2,1)}, u32[]{:S(2)}, u32[]{:S(2)}) %collective-permute-start.1) | collective-permute-done | bytes 786464 | tf_op jit(solution)/shard_map/ppermute | solution.py:14
  35.2 41.9 %all-gather.4.cloned.1.call-done = bf16[256,2,3072]{2,0,1:T(8,128)(2,1)} async-done(((bf16[64,2,3072]{2,0,1:T(8,128)(2,1)}), bf16[256,2,3072]{2,0,1:T(8,128)(2,1)}) %all-gather.4.cloned.1.call-update) | async-done | bytes 3145744 | tf_op jit(solution)/shard_map/all_gather | solution.py:38
  77.1 37.7 %all-gather.6.cloned.1.call-done = bf16[3072,1,768]{2,0,1:T(8,128)(2,1)} async-done(((bf16[768,1,768]{2,0,1:T(8,128)(2,1)}), bf16[3072,1,768]{2,0,1:T(8,128)(2,1)}) %all-gather.6.cloned.1.call-update) | async-done | bytes 4718608 | tf_op jit(solution)/shard_map/all_gather | solution.py:42
  114.7 5.9 %fusion = f32[256,2,768]{2,0,1:T(8,128)S(1)} fusion(bf16[256,2,3072]{2,0,1:T(8,128)(2,1)} %all-gather.4.cloned.1.call-done, bf16[3072,1,768]{2,0,1:T(8,128)(2,1)} %all-gather.6.cloned.1.call-done), kind=kOutput, calls=%fused_computation | convolution fusion | flops 2415919104 | bytes 9437184 | tf_op jit(solution)/shard_map/qye,ea->qya/dot_general | solution.py:39
  120.9 1.7 fusion.13
  122.6 0.4 multiply_reduce_fusion.1
  123.0 0.5 fusion.32
  123.8 0.4 broadcast_in_dim.2
  124.2 0.7 copy-done.3
  124.9 0.6 convolution_dynamic-update-slice_fusion.3
  125.5 0.6 copy-done.5
  126.1 0.6 convolution_dynamic-update-slice_fusion.2
  126.7 1.7 convolution_dynamic-update-slice_fusion.1
  128.4 1.7 convolution_dynamic-update-slice_fusion
  130.1 1.6 copy-done
  131.8 60.6 %reduce-scatter.2.cloned.1.call-done = bf16[64,2,3072]{2,0,1:T(8,128)(2,1)} async-done(((bf16[256,2,3072]{2,0,1:T(8,128)(2,1)}), bf16[64,2,3072]{2,0,1:T(8,128)(2,1)}) %reduce-scatter.2.cloned.1.call-update) | async-done | bytes 786448 | tf_op jit(solution)/shard_map/reduce_scatter | solution.py:70
  192.3 1.6 fusion.7
  193.9 1.7 copy.11
  (30 shorter events, 0.7 us)
Async XLA Ops:
  6.5 2.9 %copy-start.1 = (bf16[64,2,3072]{2,1,0:T(2,128)(2,1)S(1)}, bf16[64,2,3072]{2,1,0:T(2,128)(2,1)}, u32[]{:S(2)}) copy-start(bf16[64,2,3072]{2,1,0:T(2,128)(2,1)} %param.6) | copy-start | bytes 2359300
  6.5 2.9 %copy-start.6 = (f32[3072]{0:T(1024)S(1)}, f32[3072]{0:T(1024)}, u32[]{:S(2)}) copy-start(f32[3072]{0:T(1024)} %param.7) | copy-start | bytes 36868
  6.5 70.5 %all-gather.4.cloned.1.call-start = ((), (), s32[]{:S(2)}) async-start(), calls=%async_computation.1 | async-start | bytes 3932160 | tf_op jit(solution)/shard_map/all_gather | solution.py:38
  9.5 2.1 %copy-start.2 = (bf16[1,512,768]{2,1,0:T(8,128)(2,1)S(1)}, bf16[1,512,768]{2,1,0:T(8,128)(2,1)}, u32[]{:S(2)}) copy-start(bf16[1,512,768]{2,1,0:T(8,128)(2,1)} %param.11) | copy-start | bytes 2359300
  10.7 104.0 %all-gather.6.cloned.1.call-start = ((), (), s32[]{:S(2)}) async-start(), calls=%async_computation.3 | async-start | bytes 5898240 | tf_op jit(solution)/shard_map/all_gather | solution.py:42
  11.5 180.9 %reduce-scatter.2.cloned.1.call-start = ((), (), s32[]{:S(2)}) async-start(), calls=%async_computation.2 | async-start | bytes 3932160 | tf_op jit(solution)/shard_map/reduce_scatter | solution.py:70
  11.5 12.1 %collective-permute-start = (bf16[512,768]{1,0:T(8,128)(2,1)S(1)}, bf16[512,768]{1,0:T(8,128)(2,1)S(1)}, u32[]{:S(2)}, u32[]{:S(2)}) collective-permute-start(bf16[512,768]{1,0:T(8,128)(2,1)S(1)} %bitcast.28), channel_id=1, source_target_pairs={{0,1},{1,2},{2,3},{3,0},{4,5},{5,6},{6,7},{7,4},{8,9},{9,10},{10,1... | collective-permute-start | bytes 2359304 | tf_op jit(solution)/shard_map/ppermute | solution.py:14
  23.7 96.9 %copy-start.4 = (bf16[512,768]{1,0:T(8,128)(2,1)}, bf16[512,768]{1,0:T(8,128)(2,1)S(1)}, u32[]{:S(2)}) copy-start(bf16[512,768]{1,0:T(8,128)(2,1)S(1)} %collective-permute-done) | copy-start | bytes 2359300
  23.7 11.5 %collective-permute-start.1 = (bf16[512,768]{1,0:T(8,128)(2,1)S(1)}, bf16[512,768]{1,0:T(8,128)(2,1)}, u32[]{:S(2)}, u32[]{:S(2)}) collective-permute-start(bf16[512,768]{1,0:T(8,128)(2,1)S(1)} %collective-permute-done), channel_id=1, source_target_pairs={{0,1},{1,2},{2,3},{3,0},{4,5},{5,6},{6,7},{7,4},{8,9},{9,10},{10,1... | collective-permute-start | bytes 2359304 | tf_op jit(solution)/shard_map/ppermute | solution.py:14
  35.2 93.2 %collective-permute-start.2 = (bf16[512,768]{1,0:T(8,128)(2,1)}, bf16[512,768]{1,0:T(8,128)(2,1)}, u32[]{:S(2)}, u32[]{:S(2)}) collective-permute-start(bf16[512,768]{1,0:T(8,128)(2,1)} %collective-permute-done.1), channel_id=1, source_target_pairs={{0,1},{1,2},{2,3},{3,0},{4,5},{5,6},{6,7},{7,4},{8,9},{9,10},{10,1... | collective-permute-start | bytes 2359304 | tf_op jit(solution)/shard_map/ppermute | solution.py:14
  120.6 2.4 %copy-start.7 = (f32[1,128]{1,0:T(1,128)S(1)}, f32[1,128]{1,0:T(1,128)}, u32[]{:S(2)}) copy-start(f32[1,128]{1,0:T(1,128)} %param.10) | copy-start | bytes 1540
  120.6 2.4 %copy-start.8 = (f32[1,128]{1,0:T(1,128)S(1)}, f32[1,128]{1,0:T(1,128)}, u32[]{:S(2)}) copy-start(f32[1,128]{1,0:T(1,128)} %param.9) | copy-start | bytes 1540
  123.8 1.1 copy-start.3
  124.9 1.1 copy-start.5
  130.1 1.7 copy-start
Sparse Core Ops, SparseCore 0:
  10.9 66.1 all-gather.3
  78.6 36.0 all-gather.5
  131.9 60.3 reduce-scatter.1
